TPU v7x, 32 devices: a whole 2x2x4 slice. The times are simulated.
32 devices in a mesh: gx: 4 (over y, x), gy: 8 (over z, core).
Axes of the slice: x: 2, y: 2, z: 4, core: 2. Of those that a mesh axis runs over, the one named last changes fastest.
Arguments:
- velocity: float32 [3, 48, 224, 1024], P(None, 'gx', 'gy'), may hold values from -12 to 12
- viscosity: float32 [48, 224, 1024], P('gx', 'gy'), may hold values from 0.5 to 4
- cells: int32 [3, 32768], P(None, ('gx', 'gy')), may hold values from 0 to 1023, as said below
- offsets: float32 [3, 32768], P(None, ('gx', 'gy')), may hold values from 0 to 1
- forces: float32 [3, 32768], P(None, ('gx', 'gy')), may hold values from -48 to 48
- owners: int32 [32768, 1], P(('gx', 'gy')), may hold values from 0 to 31; in each aligned block of 1024 rows (0 to 1023, 1024 to 2047, ...) at most 64 rows name the same one
Outputs:
- new_velocity: float32 [3, 48, 224, 1024], P(None, 'gx', 'gy')
- marker_velocity: float32 [3, 32768], P(None, ('gx', 'gy'))
Inputs may be any that keep to these rules, and one draw needn't show every extreme that they name: cells[0] lies below 12, cells[1] below 28, cells[2] below 1024. `owners`: among one device's 1024 markers at most 64 have the same owner, and in every draw some owner is named exactly 64 times by one device's markers.
All inputs are finite; a program needn't handle non-finite values.
Results may differ from a plain program's by a relative error of at most 0.000096.
Values sent between devices are 32-bit elements; how exact they have to be, the bound alone decides.
A program may use at most 128 MiB of HBM per device.

v0:
```python
import functools

import jax
import jax.numpy as jnp
from jax import lax
from jax.experimental import pallas as pl
from jax.experimental.pallas import tpu as pltpu
from jax.sharding import PartitionSpec as P


MESH = pl.DeviceIdType.MESH

SWEEPS = 3
LANES = 128


def shifted(block, axis, step):
    count = lax.axis_size(axis)
    return lax.ppermute(block, axis, [(i, (i + step) % count) for i in range(count)])


def kernel_weights(frac):
    root = jnp.sqrt(1.0 + 4.0 * frac - 4.0 * frac * frac)
    return (
        (3.0 - 2.0 * frac - root) * 0.125,
        (3.0 - 2.0 * frac + root) * 0.125,
        (1.0 + 2.0 * frac + root) * 0.125,
        (1.0 + 2.0 * frac - root) * 0.125,
    )


def exchange_kernel(out_ref, in_ref, send_sem, recv_sem):
    count_x, count_y = lax.axis_size("gx"), lax.axis_size("gy")
    devices = count_x * count_y
    me = lax.axis_index("gx") * count_y + lax.axis_index("gy")

    def place(index):
        return (lax.div(index, count_y), lax.rem(index, count_y))

    barrier = pltpu.get_barrier_semaphore()

    def greet(k, carry):
        pl.semaphore_signal(
            barrier, inc=1, device_id=place(lax.rem(me + k, devices)), device_id_type=MESH
        )
        return carry

    lax.fori_loop(1, devices, greet, 0)
    pl.semaphore_wait(barrier, devices - 1)

    def copy(k, source, target):
        return pltpu.make_async_remote_copy(
            src_ref=out_ref.at[target], dst_ref=in_ref.at[source],
            send_sem=send_sem.at[k], recv_sem=recv_sem.at[k],
            device_id=place(target), device_id_type=MESH,
        )

    def begin(k, carry):
        copy(k, me, lax.rem(me + k, devices)).start()
        return carry

    def finish(k, carry):
        target = lax.rem(me + k, devices)
        source = lax.rem(me + devices - k, devices)
        copy(k, me, target).wait_send()
        copy(k, source, target).wait_recv()
        return carry

    lax.fori_loop(1, devices, begin, 0)
    in_ref[me] = out_ref[me]
    lax.fori_loop(1, devices, finish, 0)


def exchanged(values, count, collective_id):
    devices = lax.axis_size("gx") * lax.axis_size("gy")
    rows = values.shape[0]
    tile = 8 * LANES
    sized = -(-rows * count // tile) * tile
    flat = values.reshape(rows, devices, count).transpose(1, 0, 2).reshape(devices, rows * count)
    flat = jnp.pad(flat, ((0, 0), (0, sized - rows * count)))
    flat = flat.reshape(devices, sized // LANES, LANES)
    received = pl.pallas_call(
        exchange_kernel,
        out_shape=jax.ShapeDtypeStruct(flat.shape, jnp.float32),
        in_specs=[pl.BlockSpec(memory_space=pltpu.VMEM)],
        out_specs=pl.BlockSpec(memory_space=pltpu.VMEM),
        scratch_shapes=[pltpu.SemaphoreType.DMA((devices,)), pltpu.SemaphoreType.DMA((devices,))],
        compiler_params=pltpu.CompilerParams(collective_id=collective_id, has_side_effects=True),
    )(flat)
    received = received.reshape(devices, sized)[:, : rows * count].reshape(devices, rows, count)
    return received.transpose(1, 0, 2).reshape(rows, devices * count)


def tent(first, weights, length, wrap=0):
    rows = lax.broadcasted_iota(jnp.int32, (length, LANES), 0)
    table = jnp.zeros((length, LANES), jnp.float32)
    for j in range(4):
        target = first + j
        if wrap:
            target = jnp.where(target < 0, target + wrap, target)
            target = jnp.where(target >= wrap, target - wrap, target)
        table = table + jnp.where(rows == target, weights[j], 0.0)
    return table


def halves(value):
    high = value.astype(jnp.bfloat16)
    low = (value - high.astype(jnp.float32)).astype(jnp.bfloat16)
    return high, low


def chunk_tables(part, tile, x_shift, layers, ext_y, depth):
    cells = part[0:3].astype(jnp.int32)
    table_x = tent(cells[0:1] + x_shift, kernel_weights(part[3:4]), layers)
    table_y = tent(cells[1:2] - 1, kernel_weights(part[4:5]), ext_y, ext_y)
    start = cells[2:3] - 1
    start = jnp.where(start < 0, start + depth, start) - tile * LANES
    table_z = tent(start, kernel_weights(part[5:6]), 2 * LANES)
    return table_x, table_y, table_z


def chunk_count(ref):
    return jnp.max(ref[11:12, 0:LANES]).astype(jnp.int32)


def note_tiles(tables, tile_ref):
    for k, ref in enumerate(tables):
        for j in range(ref.shape[1] // LANES):
            tile = jnp.max(ref[10:11, j * LANES : (j + 1) * LANES])
            tile_ref[k, j] = tile.astype(jnp.int32)


def lanes_of(tile):
    return pl.ds(pl.multiple_of(tile * LANES, LANES), LANES)


def transposed_dot(left, right):
    return lax.dot_general(
        left, right, (((1,), (1,)), ((), ())), preferred_element_type=jnp.float32
    )


def padded(count):
    return -(-count // 8) * 8


def spread_kernel(shifts, together, *refs):
    tables, outs, tile_ref = refs[: len(shifts)], refs[len(shifts) : -1], refs[-1]

    def clear(out_ref):
        def body(i, carry):
            for c in range(3):
                out_ref[c, i] = jnp.zeros(out_ref.shape[2:], jnp.float32)
            return carry

        lax.fori_loop(0, out_ref.shape[1], body, 0)

    for out_ref in outs:
        clear(out_ref)
    note_tiles(tables, tile_ref)

    def product(which, j):
        ref, out_ref = tables[which], outs[which]
        layers, ext_y, depth = out_ref.shape[1:]
        part = ref[:, lanes_of(j)]
        table_x, table_y, table_z = chunk_tables(
            part, tile_ref[which, j], shifts[which], padded(layers), ext_y, depth
        )
        z_high, z_low = halves(table_z)
        z_pair = jnp.concatenate([z_high, z_high], axis=1)
        planes = []
        for c in range(3):
            pushed = table_x * part[6 + c : 7 + c]
            planes += [pushed[x : x + 1] * table_y for x in range(layers)]
        high, low = halves(jnp.concatenate(planes, axis=0))
        total = transposed_dot(jnp.concatenate([high, low], axis=1), z_pair)
        return total + transposed_dot(high, z_low)

    def add(which, j, total):
        out_ref = outs[which]
        layers, ext_y, depth = out_ref.shape[1:]
        shape = (3, layers, ext_y, LANES)
        tile = tile_ref[which, j]
        after = lax.rem(tile + 1, depth // LANES)
        out_ref[:, :, :, lanes_of(tile)] += total[:, :LANES].reshape(shape)
        out_ref[:, :, :, lanes_of(after)] += total[:, LANES:].reshape(shape)

    def chunk(j, carry):
        kinds = range(len(tables))
        steps = [(which, together * j + k) for which in kinds for k in range(together)]
        totals = [product(*step) for step in steps]
        for step, total in zip(steps, totals):
            add(*step, total)
        return carry

    count = chunk_count(tables[0])
    for ref in tables[1:]:
        count = jnp.maximum(count, chunk_count(ref))
    lax.fori_loop(0, lax.div(count + (together - 1), together), chunk, 0)


def spread_out(tables, shifts, layers, together, ext_y, depth, cost):
    chunks = tables[0].shape[1] // LANES
    return pl.pallas_call(
        functools.partial(spread_kernel, shifts, together),
        out_shape=[
            jax.ShapeDtypeStruct((3, count, ext_y, depth), jnp.float32) for count in layers
        ],
        in_specs=[pl.BlockSpec(memory_space=pltpu.VMEM)] * len(tables),
        out_specs=[pl.BlockSpec(memory_space=pltpu.VMEM)] * len(tables),
        scratch_shapes=[pltpu.SMEM((len(tables), chunks), jnp.int32)],
        compiler_params=pltpu.CompilerParams(vmem_limit_bytes=24 * 1024 * 1024),
        cost_estimate=pl.CostEstimate(flops=cost, bytes_accessed=1_000_000, transcendentals=0),
    )(*tables)


def smoothing_kernel(
    own_ref, below_ref, above_ref, vel_hbm, visc_hbm, vel_low, vel_high, out_ref, vel_ref,
    visc_ref, rhs_ref, field_a, field_b, fold_send, fold_recv, x_send, x_recv, y_send, y_recv,
    last_send, last_recv, load_sem, send_sem, recv_sem
):
    size_x, size_y, depth = visc_hbm.shape
    ext_y = out_ref.shape[2]
    layers = size_x + 2
    tiles = depth // LANES
    count_x, count_y = lax.axis_size("gx"), lax.axis_size("gy")
    me_x, me_y = lax.axis_index("gx"), lax.axis_index("gy")
    x_up = (lax.rem(me_x + 1, count_x), me_y)
    x_down = (lax.rem(me_x + count_x - 1, count_x), me_y)
    y_up = (me_x, lax.rem(me_y + 1, count_y))
    y_down = (me_x, lax.rem(me_y + count_y - 1, count_y))

    loads = [
        pltpu.make_async_copy(source, target, load_sem.at[k])
        for k, (source, target) in enumerate(
            (
                (vel_low, vel_ref.at[:, 0:1]),
                (vel_high, vel_ref.at[:, size_x + 1 :]),
                (vel_hbm, vel_ref.at[:, 1 : size_x + 1]),
                (visc_hbm, visc_ref),
            )
        )
    ]
    for copy in loads:
        copy.start()

    barrier = pltpu.get_barrier_semaphore()
    for device in (x_up, x_down, y_up, y_down):
        pl.semaphore_signal(barrier, inc=1, device_id=device, device_id_type=MESH)
    pl.semaphore_wait(barrier, 4)

    used = [0]

    def send(source, target, device):
        sem = used[0]
        used[0] = sem + 1
        copy = pltpu.make_async_remote_copy(
            src_ref=source, dst_ref=target, send_sem=send_sem.at[sem], recv_sem=recv_sem.at[sem],
            device_id=device, device_id_type=MESH,
        )
        copy.start()
        return copy

    def wait(copies):
        for copy in copies:
            copy.wait()

    def row_of(ref, *index):
        return jnp.concatenate([ref[(*index, slice(t, t + 1))] for t in range(tiles)], axis=1)

    def set_row(ref, value, *index):
        for t in range(tiles):
            ref[(*index, slice(t, t + 1))] = value[:, t * LANES : (t + 1) * LANES]

    def build(x, beside=None, at=0):
        for c in range(3):
            plane = own_ref[c, x]
            if beside is not None:
                plane = plane + beside[c, x - at]
            inner = plane[0:size_y] + vel_ref[c, x]
            rhs_ref[c, x, size_y:ext_y, :] = plane[size_y:ext_y]
            rhs_ref[c, x, 0:size_y, :] = inner
            set_row(fold_send, inner[size_y - 1 : size_y], x, 0, c)
            set_row(fold_send, plane[size_y : size_y + 1], x, 1, c)
            set_row(fold_send, plane[size_y + 1 : size_y + 2], x, 2, c)
            set_row(fold_send, plane[ext_y - 1 : ext_y], x, 3, c)
            set_row(fold_send, inner[0:1], x, 4, c)

    def send_fold(first, count):
        part = pl.ds(first, count)
        return (
            send(fold_send.at[part, 0:3], fold_recv.at[part, 0:3], y_up),
            send(fold_send.at[part, 3:5], fold_recv.at[part, 3:5], y_down),
        )

    def fold(x, carry):
        for c in range(3):
            rhs_ref[c, x, 0:1, :] += row_of(fold_recv, x, 1, c)
            rhs_ref[c, x, 1:2, :] += row_of(fold_recv, x, 2, c)
            rhs_ref[c, x, size_y - 1 : size_y, :] += row_of(fold_recv, x, 3, c)
            rhs_ref[c, x, ext_y - 1 : ext_y, :] += row_of(fold_recv, x, 0, c)
            rhs_ref[c, x, size_y : size_y + 1, :] += row_of(fold_recv, x, 4, c)
        return carry

    below, above = below_ref.shape[1], above_ref.shape[1]

    def lower(x, carry):
        build(x, below_ref, 0)
        return carry

    def middle(x, carry):
        build(x)
        return carry

    def upper(x, carry):
        build(x, above_ref, layers - above)
        return carry

    wait(loads)
    lax.fori_loop(0, below, lower, 0)
    low_fold = send_fold(0, 3)
    lax.fori_loop(layers - above, layers, upper, 0)
    middle(layers - 3, 0)
    high_fold = send_fold(layers - 3, 3)
    lax.fori_loop(3, layers - 3, middle, 0)
    middle_fold = send_fold(3, layers - 6)

    def update(sweep, x, low=None, high=None, edge=None):
        visc = visc_ref[x]
        scale = 1.0 / (1.0 + 6.0 * visc)
        shift = 1 if sweep == 0 else 0
        current = (rhs_ref, field_a, field_b)[sweep]
        for c in range(3):
            wide = current[c, x + shift]
            total = pltpu.roll(wide, 1, 0) + pltpu.roll(wide, ext_y - 1, 0)
            total = total + pltpu.roll(wide, 1, 1) + pltpu.roll(wide, depth - 1, 1)
            before = current[c, x + shift - 1, 0:size_y, :] if low is None else x_recv[low, c]
            behind = current[c, x + shift + 1, 0:size_y, :] if high is None else x_recv[high, c]
            total = total[0:size_y] + before + behind
            plane = (rhs_ref[c, x + 1, 0:size_y, :] + visc * total) * scale
            if sweep == SWEEPS - 1:
                out_ref[c, x, 0:size_y, :] = plane
                set_row(last_send, plane[size_y - 1 : size_y], 0, x, c)
                set_row(last_send, plane[0:1], 1, x, c)
                set_row(last_send, plane[1:2], 2, x, c)
            else:
                (field_a, field_b)[sweep][c, x, 0:size_y, :] = plane
                set_row(y_send, plane[size_y - 1 : size_y], sweep, 0, x, c)
                set_row(y_send, plane[0:1], sweep, 1, x, c)
                if edge is not None:
                    x_send[2 * sweep + edge, c] = plane

    def interior(sweep):
        def body(x, carry):
            update(sweep, x)
            return carry

        lax.fori_loop(1, size_x - 1, body, 0)

    def send_x(sweep, way):
        slot = 2 * sweep + way
        return send(x_send.at[slot], x_recv.at[slot], (x_up, x_down)[way])

    def send_y(sweep, first, count):
        part = pl.ds(first, count)
        return (
            send(y_send.at[sweep, 0, part], y_recv.at[sweep, 0, part], y_up),
            send(y_send.at[sweep, 1, part], y_recv.at[sweep, 1, part], y_down),
        )

    def send_last(first, count):
        part = pl.ds(first, count)
        return (
            send(last_send.at[0, part], last_recv.at[0, part], y_up),
            send(last_send.at[1:3, part], last_recv.at[1:3, part], y_down),
        )

    def halo(sweep):
        field = (field_a, field_b)[sweep]

        def body(x, carry):
            for c in range(3):
                field[c, x, size_y : size_y + 1, :] = row_of(y_recv, sweep, 1, x, c)
                field[c, x, ext_y - 1 : ext_y, :] = row_of(y_recv, sweep, 0, x, c)
            return carry

        lax.fori_loop(0, size_x, body, 0)

    def halo_last(x, carry):
        for c in range(3):
            out_ref[c, x, size_y : size_y + 1, :] = row_of(last_recv, 1, x, c)
            out_ref[c, x, size_y + 1 : size_y + 2, :] = row_of(last_recv, 2, x, c)
            out_ref[c, x, size_y + 2 : ext_y - 1, :] = jnp.zeros(
                (ext_y - 3 - size_y, depth), jnp.float32
            )
            out_ref[c, x, ext_y - 1 : ext_y, :] = row_of(last_recv, 0, x, c)
        return carry

    wait(low_fold)
    lax.fori_loop(0, 3, fold, 0)
    update(0, 0, edge=1)
    x_copies = (send_x(0, 1),)
    wait(high_fold)
    lax.fori_loop(layers - 3, layers, fold, 0)
    update(0, size_x - 1, edge=0)
    x_copies = x_copies + (send_x(0, 0),)
    wait(middle_fold)
    lax.fori_loop(3, layers - 3, fold, 0)
    interior(0)
    y_copies = send_y(0, 0, size_x)
    wait(y_copies)
    halo(0)
    interior(1)
    y_copies = send_y(1, 1, size_x - 2)
    wait(x_copies)
    update(1, 0, low=0, edge=1)
    x_copies = (send_x(1, 1),)
    update(1, size_x - 1, high=1, edge=0)
    x_copies = x_copies + (send_x(1, 0),)
    y_copies = y_copies + send_y(1, 0, 1) + send_y(1, size_x - 1, 1)
    wait(y_copies)
    halo(1)
    interior(2)
    y_copies = send_last(1, size_x - 2)
    wait(y_copies)
    lax.fori_loop(1, size_x - 1, halo_last, 0)
    wait(x_copies)
    update(2, 0, low=2)
    y_copies = send_last(0, 1)
    update(2, size_x - 1, high=3)
    y_copies = y_copies + send_last(size_x - 1, 1)
    wait(y_copies)
    halo_last(0, 0)
    halo_last(size_x - 1, 0)


def smoothed(own, below, above, velocity, viscosity, vel_low, vel_high):
    size_x, size_y, depth = viscosity.shape
    ext_y = own.shape[2]
    layers = size_x + 2
    tiles = depth // LANES
    f32 = jnp.float32
    vmem, hbm = pl.BlockSpec(memory_space=pltpu.VMEM), pl.BlockSpec(memory_space=pl.ANY)
    return pl.pallas_call(
        smoothing_kernel,
        out_shape=jax.ShapeDtypeStruct((3, size_x, ext_y, depth), f32),
        in_specs=[vmem] * 3 + [hbm] * 4,
        out_specs=vmem,
        scratch_shapes=[
            pltpu.VMEM((3, layers, size_y, depth), f32),
            pltpu.VMEM((size_x, size_y, depth), f32),
            pltpu.VMEM((3, layers, ext_y, depth), f32),
            pltpu.VMEM((3, size_x, ext_y, depth), f32),
            pltpu.VMEM((3, size_x, ext_y, depth), f32),
            pltpu.VMEM((layers, 5, 3, tiles, LANES), f32),
            pltpu.VMEM((layers, 5, 3, tiles, LANES), f32),
            pltpu.VMEM((4, 3, size_y, depth), f32),
            pltpu.VMEM((4, 3, size_y, depth), f32),
            pltpu.VMEM((2, 2, size_x, 3, tiles, LANES), f32),
            pltpu.VMEM((2, 2, size_x, 3, tiles, LANES), f32),
            pltpu.VMEM((3, size_x, 3, tiles, LANES), f32),
            pltpu.VMEM((3, size_x, 3, tiles, LANES), f32),
            pltpu.SemaphoreType.DMA((4,)),
            pltpu.SemaphoreType.DMA((24,)),
            pltpu.SemaphoreType.DMA((24,)),
        ],
        compiler_params=pltpu.CompilerParams(
            collective_id=0, has_side_effects=True, vmem_limit_bytes=36 * 1024 * 1024
        ),
    )(own, below, above, velocity, viscosity, vel_low, vel_high)


def sample_chunk(ref, tile, j, target, x_shift, high_of, low_of):
    layers, ext_y, depth = high_of.shape[1:]
    after = lax.rem(tile + 1, depth // LANES)
    table_x, table_y, table_z = chunk_tables(
        ref[:, lanes_of(j)], tile, x_shift, padded(layers), ext_y, depth
    )
    z_high, z_low = halves(table_z)
    z_pair = jnp.concatenate([z_high, z_low], axis=1)

    def window(ref):
        rows = (3 * layers * ext_y, LANES)
        return jnp.concatenate(
            [
                ref[:, :, :, lanes_of(tile)].reshape(rows),
                ref[:, :, :, lanes_of(after)].reshape(rows),
            ],
            axis=1,
        )

    pair = jnp.dot(window(high_of), z_pair, preferred_element_type=jnp.float32)
    columns = pair[:, :LANES] + pair[:, LANES:]
    columns = columns + jnp.dot(window(low_of), z_high, preferred_element_type=jnp.float32)
    for c in range(3):
        total = jnp.zeros((8, LANES), jnp.float32)
        for x in range(layers):
            at = (c * layers + x) * ext_y
            weighted = columns[at : at + ext_y] * table_y
            summed = weighted[0:8]
            for k in range(8, ext_y, 8):
                summed = summed + weighted[k : k + 8]
            total = total + summed * table_x[x : x + 1]
        target[c : c + 1, lanes_of(j)] = jnp.sum(total, axis=0, keepdims=True)


def sample_kernel(table_ref, field_ref, vel_ref, out_ref, field_high, field_low, tile_ref):
    size_x, size_y = vel_ref.shape[1:3]

    def split(x, carry):
        for c in range(3):
            plane = field_ref[c, x]
            vel_ref[c, x] = plane[0:size_y]
            field_high[c, x], field_low[c, x] = halves(plane)
        return carry

    lax.fori_loop(0, size_x, split, 0)
    note_tiles([table_ref], tile_ref)

    def chunk(i, carry):
        for j in (2 * i, 2 * i + 1):
            sample_chunk(table_ref, tile_ref[0, j], j, out_ref, -1, field_high, field_low)
        return carry

    lax.fori_loop(0, lax.div(chunk_count(table_ref) + 1, 2), chunk, 0)


def sampled(table, field, size_y):
    size_x, ext_y, depth = field.shape[1:]
    f32 = jnp.float32
    vmem = pl.BlockSpec(memory_space=pltpu.VMEM)
    return pl.pallas_call(
        sample_kernel,
        out_shape=(
            jax.ShapeDtypeStruct((3, size_x, size_y, depth), f32),
            jax.ShapeDtypeStruct((3, table.shape[1]), f32),
        ),
        in_specs=[vmem] * 2,
        out_specs=[vmem] * 2,
        scratch_shapes=[pltpu.VMEM((3, size_x, ext_y, depth), jnp.bfloat16)] * 2
        + [pltpu.SMEM((1, table.shape[1] // LANES), jnp.int32)],
        compiler_params=pltpu.CompilerParams(vmem_limit_bytes=28 * 1024 * 1024),
        cost_estimate=pl.CostEstimate(
            flops=10_000_000_000, bytes_accessed=1_000_000, transcendentals=0
        ),
    )(table, field)


def sample_beside_kernel(
    low_ref, high_ref, field_ref, low_out, high_out, first_high, first_low, last_high, last_low,
    tile_ref
):
    size_x = field_ref.shape[1]
    for c in range(3):
        for x in range(2):
            first_high[c, x], first_low[c, x] = halves(field_ref[c, x])
        last_high[c, 0], last_low[c, 0] = halves(field_ref[c, size_x - 1])
    note_tiles([low_ref, high_ref], tile_ref)

    def chunk(j, carry):
        sample_chunk(
            low_ref, tile_ref[0, j], j, low_out, -size_x - 1, first_high, first_low
        )
        sample_chunk(high_ref, tile_ref[1, j], j, high_out, 0, last_high, last_low)
        return carry

    lax.fori_loop(0, jnp.maximum(chunk_count(low_ref), chunk_count(high_ref)), chunk, 0)


def sampled_beside(low, high, field):
    ext_y, depth = field.shape[2:]
    vmem = pl.BlockSpec(memory_space=pltpu.VMEM)
    return pl.pallas_call(
        sample_beside_kernel,
        out_shape=[jax.ShapeDtypeStruct((3, low.shape[1]), jnp.float32)] * 2,
        in_specs=[vmem] * 3,
        out_specs=[vmem] * 2,
        scratch_shapes=[pltpu.VMEM((3, 2, ext_y, depth), jnp.bfloat16)] * 2
        + [pltpu.VMEM((3, 1, ext_y, depth), jnp.bfloat16)] * 2
        + [pltpu.SMEM((2, low.shape[1] // LANES), jnp.int32)],
        compiler_params=pltpu.CompilerParams(vmem_limit_bytes=16 * 1024 * 1024),
        cost_estimate=pl.CostEstimate(
            flops=2_000_000_000, bytes_accessed=1_000_000, transcendentals=0
        ),
    )(low, high, field)


def ranked(onehot):
    members, kinds = onehot.shape
    group = min(128, members)
    blocks = onehot.reshape(members // group, group, kinds)
    lower = (
        lax.broadcasted_iota(jnp.int32, (group, group), 0)
        > lax.broadcasted_iota(jnp.int32, (group, group), 1)
    ).astype(jnp.float32)
    within = jnp.einsum("ij,bjd->bid", lower, blocks)
    totals = jnp.sum(blocks, axis=1)
    before = jnp.cumsum(totals, axis=0) - totals
    rank = jnp.sum((within + before[:, None, :]) * blocks, axis=-1).reshape(members)
    return rank.astype(jnp.int32), jnp.sum(totals, axis=0).astype(jnp.int32)


def onehot_of(index, kinds):
    return (index[:, None] == lax.broadcasted_iota(jnp.int32, (index.shape[0], kinds), 1)).astype(
        jnp.float32
    )


def stepped(velocity, viscosity, cells, offsets, forces, owners):
    rows_gx = lax.axis_size("gx")
    rows_gy = lax.axis_size("gy")
    devices = rows_gx * rows_gy
    markers = owners.shape[0]
    capacity = max(2, 2 * markers // devices)
    slots = capacity * devices
    size_x, size_y, depth = viscosity.shape
    ext_y = -(-(size_y + 3) // 8) * 8
    tiles = depth // LANES

    owner = owners[:, 0]
    rank, _ = ranked(onehot_of(owner, devices))
    slot = owner * capacity + rank
    payload = jnp.concatenate(
        [cells.astype(jnp.float32), offsets, forces, jnp.ones((1, markers), jnp.float32)], axis=0
    )
    outgoing = jnp.zeros((10, slots), jnp.float32).at[:, slot].set(payload, unique_indices=True)
    received = exchanged(outgoing, capacity, 1)
    edges = (velocity[:, size_x - 1 :], velocity[:, 0:1])
    received, edges = lax.optimization_barrier((received, edges))
    vel_low = shifted(edges[0], "gx", 1)
    vel_high = shifted(edges[1], "gx", -1)

    valid = received[9] > 0.5
    start = received[2].astype(jnp.int32) - 1
    bins = jnp.where(start < 0, start + depth, start) // LANES
    bins = jnp.where(valid, bins, tiles)
    chunks = -(-(slots // LANES + tiles) // 2) * 2
    places = chunks * LANES
    rank, totals = ranked(onehot_of(bins, tiles))
    needed = (totals + (LANES - 1)) // LANES
    ends = jnp.cumsum(needed)
    first = ends - needed
    shift = jnp.sum(jnp.where(bins[:, None] == jnp.arange(tiles)[None, :], first[None, :], 0), axis=1)
    spot = jnp.where(valid, shift * LANES + rank, places)
    count = jnp.full((slots,), ends[-1].astype(jnp.float32))
    sorting = jnp.concatenate([received, jnp.stack([bins.astype(jnp.float32), count])], axis=0)
    own = jnp.zeros((12, places), jnp.float32).at[:, spot].set(
        sorting, mode="drop", unique_indices=True
    )
    low = shifted(own, "gx", 1)
    high = shifted(own, "gx", -1)

    (spread,) = spread_out([own], (0,), (size_x + 2,), 2, ext_y, depth, 10_000_000_000)
    below, above = spread_out(
        [low, high], (-size_x, 0), (3, 2), 1, ext_y, depth, 2_000_000_000,
    )
    field = smoothed(spread, below, above, velocity, viscosity, vel_low, vel_high)
    low_values, high_values = sampled_beside(low, high, field)
    low_values = shifted(low_values, "gx", -1)
    high_values = shifted(high_values, "gx", 1)
    new_velocity, values = sampled(own, field, size_y)
    values = values + low_values + high_values
    back = values[:, jnp.minimum(spot, places - 1)]
    back = jnp.where(valid[None], back, 0.0)
    returned = exchanged(back, capacity, 2)
    return (new_velocity, returned[:, slot])


def solution(mesh):
    in_specs = (
        P(None, "gx", "gy", None),
        P("gx", "gy", None),
        P(None, ("gx", "gy")),
        P(None, ("gx", "gy")),
        P(None, ("gx", "gy")),
        P(("gx", "gy"), None),
    )
    out_specs = (P(None, "gx", "gy", None), P(None, ("gx", "gy")))
    return jax.shard_map(stepped, mesh=mesh, in_specs=in_specs, out_specs=out_specs, check_vma=False)
```

profile of v0, /device:TPU:0, one launch (start us, length us, event | category | flops | bytes accessed | tf_op | source)
XLA Modules:
  0.0 162.1 jit_solution(1027487918317142487)
XLA Ops:
  0.6 0.8 convert_reduce_fusion
  1.5 1.0 fusion.2
  2.4 0.7 compare_select_fusion.3
  3.1 0.7 convert_element_type.86
  3.9 0.1 pad.16.clone
  3.9 0.8 maximum_bitcast_fusion.1
  4.7 0.2 copy.42
  5.0 3.3 %scatter_custom_fusion = f32[10,2048]{0,1:T(8,128)S(1)} fusion(s32[1024]{0:T(1024)S(1)} %bitcast.100, f32[1024,10]{1,0:T(8,128)S(1)} %copy.42, f32[]{:T(128)} %constant.53.clone.1), kind=kCustom, calls=%fused_computation.14 | custom fusion | bytes 81924 | tf_op jit(solution)/shard_map/scatter | solution.py:626
  8.3 0.4 copy.43
  8.7 0.1 reshape.306
  8.8 0.7 copy.54
  9.5 13.3 %shard_map.77 = f32[32,8,128]{2,1,0:T(8,128)} custom-call(f32[32,8,128]{2,1,0:T(8,128)} %bitcast.84), custom_call_target="tpu_custom_call" | custom-call | tf_op jit(solution)/shard_map/pallas_call | solution.py:82
  22.8 0.9 copy.61
  23.8 0.1 reshape.309
  23.9 0.1 copy.44
  23.9 0.1 reshape.310
  24.0 1.9 %fusion.22 = (f32[3,1,28,1024]{3,2,1,0:T(8,128)S(1)}, f32[3,1,28,1024]{3,2,1,0:T(8,128)}) fusion(f32[3,12,28,1024]{3,2,1,0:T(8,128)} %vel_hbm.1), kind=kLoop, calls=%fused_computation.81 | loop fusion | bytes 1376256 | tf_op jit(solution)/shard_map/slice | solution.py:628
  26.0 0.1 select_convert_fusion
  26.1 0.1 convert_reduce_fusion.1
  26.3 0.2 reduce-window.4
  26.5 0.6 slice.27
  27.1 0.2 fusion.5
  27.3 0.1 select_reduce_fusion
  28.0 0.1 pad.12.clone
  28.1 0.1 maximum_bitcast_fusion
  28.2 0.4 copy.45
  28.6 6.0 %scatter_custom_fusion.1 = f32[12,3072]{0,1:T(8,128)S(1)} fusion(s32[2048]{0:T(1024)S(1)} %bitcast.103, f32[2048,12]{1,0:T(8,128)S(1)} %copy.45, f32[]{:T(128)} %constant.53.clone.1), kind=kCustom, calls=%fused_computation.12 | custom fusion | bytes 147460 | tf_op jit(solution)/shard_map/scatter | solution.py:647
  34.6 0.0 copy-start.3
  34.6 0.5 copy.49.refs_0_.table_ref
  35.1 1.3 collective-permute-start
  36.4 1.6 collective-permute-start.1
  38.0 0.0 copy-done.3
  38.0 0.4 collective-permute-start.2
  38.5 2.5 %collective-permute-start.3 = (f32[3,1,28,1024]{3,2,1,0:T(8,128)S(1)}, f32[3,1,28,1024]{3,2,1,0:T(8,128)S(1)}, u32[]{:S(2)}, u32[]{:S(2)}) collective-permute-start(f32[3,1,28,1024]{3,2,1,0:T(8,128)S(1)} %get-tuple-element.15), channel_id=1, source_target_pairs={{0,24},{8,0},{16,8},{24,16},{1,25},{9,1},{17,9},{25,17},{2,26},{10... | collective-permute-start | bytes 1032200 | tf_op jit(solution)/shard_map/ppermute | solution.py:19
  41.0 6.9 %shard_map.78.own_ref = f32[3,14,32,1024]{3,2,1,0:T(8,128)S(1)} custom-call(f32[12,3072]{1,0:T(8,128)S(1)} %copy.49.refs_0_.table_ref), custom_call_target="tpu_custom_call" | custom-call | flops 10000000000 | bytes 1000000 | tf_op jit(solution)/shard_map/pallas_call | solution.py:204
  47.9 0.0 copy-start.1
  47.9 2.4 %copy-done.1 = f32[3,14,32,1024]{3,2,1,0:T(8,128)} copy-done((f32[3,14,32,1024]{3,2,1,0:T(8,128)}, f32[3,14,32,1024]{3,2,1,0:T(8,128)S(1)}, u32[]{:S(2)}) %copy-start.1) | copy-done | bytes 5505048
  50.2 0.1 broadcast_in_dim.66
  50.3 0.0 copy-start.2
  50.3 0.0 collective-permute-done.refs_0_.low_ref
  50.4 0.0 collective-permute-done.1.refs_1_.high_ref
  50.4 9.2 %shard_map.79 = (f32[3,3,32,1024]{3,2,1,0:T(8,128)S(1)}, f32[3,2,32,1024]{3,2,1,0:T(8,128)S(1)}) custom-call(f32[12,3072]{1,0:T(8,128)S(1)} %collective-permute-done.refs_0_.low_ref, f32[12,3072]{1,0:T(8,128)S(1)} %collective-permute-done.1.refs_1_.high_ref), custom_call_target="tpu_custom_call" | custom-call | flops 2000000000 | bytes 1000000 | tf_op jit(solution)/shard_map/pallas_call | solution.py:204
  59.5 0.0 collective-permute-done.2.vel_low
  59.6 3.7 %collective-permute-done.3.vel_high = f32[3,1,28,1024]{3,2,1,0:T(8,128)S(1)} collective-permute-done((f32[3,1,28,1024]{3,2,1,0:T(8,128)S(1)}, f32[3,1,28,1024]{3,2,1,0:T(8,128)S(1)}, u32[]{:S(2)}, u32[]{:S(2)}) %collective-permute-start.3) | collective-permute-done | bytes 344096 | tf_op jit(solution)/shard_map/ppermute | solution.py:19
  63.3 0.0 copy-done.2
  63.3 2.3 %copy-done = f32[3,12,28,1024]{3,2,1,0:T(8,128)S(1)} copy-done((f32[3,12,28,1024]{3,2,1,0:T(8,128)S(1)}, f32[3,12,28,1024]{3,2,1,0:T(8,128)}, u32[]{:S(2)}) %copy-start) | copy-done | bytes 4128792
  65.6 53.9 %shard_map.80.field_ref = f32[3,12,32,1024]{3,2,1,0:T(8,128)S(1)} custom-call(f32[3,14,32,1024]{3,2,1,0:T(8,128)} %copy-done.1, f32[3,3,32,1024]{3,2,1,0:T(8,128)S(1)} %get-tuple-element.12.below_ref, f32[3,2,32,1024]{3,2,1,0:T(8,128)S(1)} %get-tuple-element.13.above_ref, f32[3,12,28,1024]{3,2,1,0:T(8,128)S(1)} %copy-done, f32[12,28,1024]{2,1,0:T(8,128)S(1)} %copy-done.2, ...), custom_call_target="tpu_custom_call" | custom-call | tf_op jit(solution)/shard_map/pallas_call | solution.py:444
  119.5 6.4 %shard_map.82 = (f32[3,3072]{1,0:T(4,128)S(1)}, f32[3,3072]{1,0:T(4,128)S(1)}) custom-call(f32[12,3072]{1,0:T(8,128)S(1)} %collective-permute-done.refs_0_.low_ref, f32[12,3072]{1,0:T(8,128)S(1)} %collective-permute-done.1.refs_1_.high_ref, f32[3,12,32,1024]{3,2,1,0:T(8,128)S(1)} %shard_map.80.field_ref), custom_call_target="tpu_custom_call" | custom-call | flops 2000000000 | bytes 1000000 | tf_op jit(solution)/shard_map/pallas_call | solution.py:573
  125.9 1.4 collective-permute-start.4
  127.4 0.8 collective-permute-start.5
  128.2 6.7 %shard_map.81 = (f32[3,12,28,1024]{3,2,1,0:T(8,128)}, f32[3,3072]{1,0:T(4,128)S(1)}) custom-call(f32[12,3072]{1,0:T(8,128)S(1)} %copy.49.refs_0_.table_ref, f32[3,12,32,1024]{3,2,1,0:T(8,128)S(1)} %shard_map.80.field_ref), custom_call_target="tpu_custom_call" | custom-call | flops 10000000000 | bytes 1000000 | tf_op jit(solution)/shard_map/pallas_call | solution.py:532
  134.9 0.0 collective-permute-done.4
  134.9 0.0 collective-permute-done.5
  134.9 0.5 copy.50
  135.4 5.5 %gather_fusion = f32[2048,3]{1,0:T(8,128)S(1)} fusion(f32[3,3072]{0,1:T(8,128)S(1)} %copy.50, s32[2048]{0:T(1024)S(1)} %broadcast_clamp_fusion), kind=kCustom, calls=%fused_computation | custom fusion | bytes 57344 | tf_op jit(solution)/shard_map/gather | solution.py:663
  140.9 0.4 copy.51
  141.3 0.1 reshape.312
  141.4 0.7 copy.56
  142.1 14.9 %shard_map.83 = f32[32,8,128]{2,1,0:T(8,128)} custom-call(f32[32,8,128]{2,1,0:T(8,128)} %bitcast.86), custom_call_target="tpu_custom_call" | custom-call | tf_op jit(solution)/shard_map/pallas_call | solution.py:82
  157.1 0.9 copy.60
  158.0 0.1 reshape.315
  158.1 0.4 copy.52
  158.5 2.8 %gather_fusion.1 = f32[1024,3]{1,0:T(8,128)S(1)} fusion(f32[3,2048]{0,1:T(8,128)S(1)} %bitcast.79, s32[1024]{0:T(1024)S(1)} %broadcast_clamp_fusion.1), kind=kCustom, calls=%fused_computation.1 | custom fusion | bytes 28672 | tf_op jit(solution)/shard_map/gather | solution.py:666
  161.3 0.8 copy.53
  (22 shorter events, 0.3 us)
Async XLA Ops:
  34.6 3.4 %copy-start.3 = (f32[3,1,28,1024]{3,2,1,0:T(8,128)S(1)}, f32[3,1,28,1024]{3,2,1,0:T(8,128)}, u32[]{:S(2)}) copy-start(f32[3,1,28,1024]{3,2,1,0:T(8,128)} %get-tuple-element.14) | copy-start | bytes 1032196
  35.1 15.3 %collective-permute-start = (f32[12,3072]{1,0:T(8,128)S(1)}, f32[12,3072]{1,0:T(8,128)S(1)}, u32[]{:S(2)}, u32[]{:S(2)}) collective-permute-start(f32[12,3072]{1,0:T(8,128)S(1)} %copy.49.refs_0_.table_ref), channel_id=1, source_target_pairs={{0,8},{8,16},{16,24},{24,0},{1,9},{9,17},{17,25},{25,1},{2,10},{10... | collective-permute-start | bytes 442376 | tf_op jit(solution)/shard_map/ppermute | solution.py:19
  36.4 13.9 %collective-permute-start.1 = (f32[12,3072]{1,0:T(8,128)S(1)}, f32[12,3072]{1,0:T(8,128)S(1)}, u32[]{:S(2)}, u32[]{:S(2)}) collective-permute-start(f32[12,3072]{1,0:T(8,128)S(1)} %copy.49.refs_0_.table_ref), channel_id=1, source_target_pairs={{0,24},{8,0},{16,8},{24,16},{1,25},{9,1},{17,9},{25,17},{2,26},{10... | collective-permute-start | bytes 442376 | tf_op jit(solution)/shard_map/ppermute | solution.py:19
  38.0 21.5 %collective-permute-start.2 = (f32[3,1,28,1024]{3,2,1,0:T(8,128)S(1)}, f32[3,1,28,1024]{3,2,1,0:T(8,128)S(1)}, u32[]{:S(2)}, u32[]{:S(2)}) collective-permute-start(f32[3,1,28,1024]{3,2,1,0:T(8,128)S(1)} %copy-done.3), channel_id=1, source_target_pairs={{0,8},{8,16},{16,24},{24,0},{1,9},{9,17},{17,25},{25,1},{2,10},{10... | collective-permute-start | bytes 1032200 | tf_op jit(solution)/shard_map/ppermute | solution.py:19
  38.5 24.8 %collective-permute-start.3 = (f32[3,1,28,1024]{3,2,1,0:T(8,128)S(1)}, f32[3,1,28,1024]{3,2,1,0:T(8,128)S(1)}, u32[]{:S(2)}, u32[]{:S(2)}) collective-permute-start(f32[3,1,28,1024]{3,2,1,0:T(8,128)S(1)} %get-tuple-element.15), channel_id=1, source_target_pairs={{0,24},{8,0},{16,8},{24,16},{1,25},{9,1},{17,9},{25,17},{2,26},{10... | collective-permute-start | bytes 1032200 | tf_op jit(solution)/shard_map/ppermute | solution.py:19
  47.9 2.4 %copy-start.1 = (f32[3,14,32,1024]{3,2,1,0:T(8,128)}, f32[3,14,32,1024]{3,2,1,0:T(8,128)S(1)}, u32[]{:S(2)}) copy-start(f32[3,14,32,1024]{3,2,1,0:T(8,128)S(1)} %shard_map.78.own_ref) | copy-start | bytes 16515076
  50.3 12.9 %copy-start.2 = (f32[12,28,1024]{2,1,0:T(8,128)S(1)}, f32[12,28,1024]{2,1,0:T(8,128)}, u32[]{:S(2)}) copy-start(f32[12,28,1024]{2,1,0:T(8,128)} %visc_hbm.1) | copy-start | bytes 4128772
  63.3 2.3 %copy-start = (f32[3,12,28,1024]{3,2,1,0:T(8,128)S(1)}, f32[3,12,28,1024]{3,2,1,0:T(8,128)}, u32[]{:S(2)}) copy-start(f32[3,12,28,1024]{3,2,1,0:T(8,128)} %vel_hbm.1) | copy-start | bytes 12386308
  125.9 9.0 %collective-permute-start.4 = (f32[3,3072]{1,0:T(4,128)S(1)}, f32[3,3072]{1,0:T(4,128)S(1)}, u32[]{:S(2)}, u32[]{:S(2)}) collective-permute-start(f32[3,3072]{1,0:T(4,128)S(1)} %get-tuple-element.18), channel_id=1, source_target_pairs={{0,24},{8,0},{16,8},{24,16},{1,25},{9,1},{17,9},{25,17},{2,26},{10... | collective-permute-start | bytes 110600 | tf_op jit(solution)/shard_map/ppermute | solution.py:19
  127.4 7.5 %collective-permute-start.5 = (f32[3,3072]{1,0:T(4,128)S(1)}, f32[3,3072]{1,0:T(4,128)S(1)}, u32[]{:S(2)}, u32[]{:S(2)}) collective-permute-start(f32[3,3072]{1,0:T(4,128)S(1)} %get-tuple-element.19), channel_id=1, source_target_pairs={{0,8},{8,16},{16,24},{24,0},{1,9},{9,17},{17,25},{25,1},{2,10},{10... | collective-permute-start | bytes 110600 | tf_op jit(solution)/shard_map/ppermute | solution.py:19
where the time goes:
time: 163 us; the launch traced here: 162 us
  Pallas kernels  111 us (68%)
  local copies, waits for them, and re-layouts  32.4 us (20%)
  starting transfers between devices  8.13 us (5%)
  other arithmetic  3.87 us (2%)
  waiting for transfers between devices  3.73 us (2%)
    pallas_call x1, Pallas kernels, smoothed(): pl.pallas_call(smoothing_kernel, out_shape=jax.ShapeDtypeStruct((3, size_...  53.9 us
    pallas_call x2, Pallas kernels, exchanged(): pl.pallas_call(exchange_kernel, out_shape=jax.ShapeDtypeStruct(flat.shape...  28.2 us
    pallas_call x2, Pallas kernels, spread_out(): pl.pallas_call(functools.partial(spread_kernel, shifts, together), out_sh...  16 us
    unnamed x15, local copies, waits for them, and re-layouts  8.75 us
    ppermute x6, starting transfers between devices, shifted(): lax.ppermute(block, axis, [(i, (i + step) % count) for i in range(count)])  8.13 us
    pallas_call x1, Pallas kernels, sampled(): pl.pallas_call(sample_kernel, out_shape=(jax.ShapeDtypeStruct((3, size_x,...  6.69 us
    scatter x2, local copies, waits for them, and re-layouts, stepped(): jnp.zeros((12, places), jnp.float32).at[:, spot]  6.46 us
    pallas_call x1, Pallas kernels, sampled_beside(): pl.pallas_call(sample_beside_kernel, out_shape=[jax.ShapeDtypeStruct((3,...  6.44 us
  transfers between devices with their start and end apart: 6, of which 1 were waited for; matrix products, arithmetic and copies ran while one was open for 0% of the time, Pallas kernels for 14%

commit v1 on v0

--- a/solution.py
+++ b/solution.py
@@ -12,6 +12,8 @@
 
 SWEEPS = 3
 LANES = 128
+SPREAD_BELOW = 3
+SPREAD_ABOVE = 2
 
 
 def shifted(block, axis, step):
@@ -29,66 +31,354 @@
     )
 
 
-def exchange_kernel(out_ref, in_ref, send_sem, recv_sem):
-    count_x, count_y = lax.axis_size("gx"), lax.axis_size("gy")
-    devices = count_x * count_y
-    me = lax.axis_index("gx") * count_y + lax.axis_index("gy")
-
-    def place(index):
-        return (lax.div(index, count_y), lax.rem(index, count_y))
-
-    barrier = pltpu.get_barrier_semaphore()
-
-    def greet(k, carry):
-        pl.semaphore_signal(
-            barrier, inc=1, device_id=place(lax.rem(me + k, devices)), device_id_type=MESH
-        )
-        return carry
-
-    lax.fori_loop(1, devices, greet, 0)
-    pl.semaphore_wait(barrier, devices - 1)
-
-    def copy(k, source, target):
+def thirds(value):
+    high = value.astype(jnp.bfloat16)
+    rest = value - high.astype(jnp.float32)
+    middle = rest.astype(jnp.bfloat16)
+    low = (rest - middle.astype(jnp.float32)).astype(jnp.bfloat16)
+    return jnp.concatenate([high, middle, low], axis=0)
+
+
+def rejoined(parts, rows):
+    return (parts[0:rows] + parts[rows : 2 * rows]) + parts[2 * rows : 3 * rows]
+
+
+def flags(match):
+    return jnp.where(match, 1.0, 0.0).astype(jnp.bfloat16)
+
+
+class Exchange:
+    def __init__(self, out_ref, in_ref, send_sem, recv_sem):
+        self.out_ref, self.in_ref = out_ref, in_ref
+        self.send_sem, self.recv_sem = send_sem, recv_sem
+        self.count_y = lax.axis_size("gy")
+        self.devices = lax.axis_size("gx") * self.count_y
+        self.me = lax.axis_index("gx") * self.count_y + lax.axis_index("gy")
+        self.barrier = pltpu.get_barrier_semaphore()
+
+    def place(self, index):
+        return (lax.div(index, self.count_y), lax.rem(index, self.count_y))
+
+    def other(self, k):
+        return lax.rem(self.me + k, self.devices)
+
+    def greet(self):
+        def body(k, carry):
+            pl.semaphore_signal(
+                self.barrier, inc=1, device_id=self.place(self.other(k)), device_id_type=MESH
+            )
+            return carry
+
+        lax.fori_loop(1, self.devices, body, 0)
+
+    def copy(self, k, source, target):
         return pltpu.make_async_remote_copy(
-            src_ref=out_ref.at[target], dst_ref=in_ref.at[source],
-            send_sem=send_sem.at[k], recv_sem=recv_sem.at[k],
-            device_id=place(target), device_id_type=MESH,
-        )
-
-    def begin(k, carry):
-        copy(k, me, lax.rem(me + k, devices)).start()
-        return carry
-
-    def finish(k, carry):
-        target = lax.rem(me + k, devices)
-        source = lax.rem(me + devices - k, devices)
-        copy(k, me, target).wait_send()
-        copy(k, source, target).wait_recv()
-        return carry
-
-    lax.fori_loop(1, devices, begin, 0)
-    in_ref[me] = out_ref[me]
-    lax.fori_loop(1, devices, finish, 0)
-
-
-def exchanged(values, count, collective_id):
+            src_ref=self.out_ref.at[target], dst_ref=self.in_ref.at[source],
+            send_sem=self.send_sem.at[k], recv_sem=self.recv_sem.at[k],
+            device_id=self.place(target), device_id_type=MESH,
+        )
+
+    def start(self):
+        pl.semaphore_wait(self.barrier, self.devices - 1)
+
+        def body(k, carry):
+            self.copy(k, self.me, self.other(k)).start()
+            return carry
+
+        lax.fori_loop(1, self.devices, body, 0)
+        self.in_ref[self.me] = self.out_ref[self.me]
+
+    def finish(self):
+        def body(k, carry):
+            source = lax.rem(self.me + self.devices - k, self.devices)
+            self.copy(k, self.me, self.other(k)).wait_send()
+            self.copy(k, source, self.me).wait_recv()
+            return carry
+
+        lax.fori_loop(1, self.devices, body, 0)
+
+
+def turned(value, amount):
+    return value if amount % LANES == 0 else pltpu.roll(value, amount % LANES, 1)
+
+
+def lane_between(first, last):
+    lane = lax.broadcasted_iota(jnp.int32, (8, LANES), 1)
+    return (lane >= first) & (lane < last)
+
+
+def put_tiles(out_ref, block, first, second, capacity):
+    for k in range(LANES // capacity):
+        tile = jnp.where(lane_between(0, capacity), turned(first, -k * capacity), 0.0)
+        if second is not None:
+            tile = jnp.where(
+                lane_between(capacity, 2 * capacity), turned(second, capacity - k * capacity), tile
+            )
+        out_ref[block * (LANES // capacity) + k] = tile
+
+
+def block_of(in_ref, block, capacity, half):
+    total = jnp.zeros((8, LANES), jnp.float32)
+    for k in range(LANES // capacity):
+        tile = in_ref[block * (LANES // capacity) + k]
+        total = jnp.where(
+            lane_between(k * capacity, (k + 1) * capacity),
+            turned(tile, (k - half) * capacity),
+            total,
+        )
+    return total
+
+
+def route_kernel(
+    capacity, owner_hbm, cells_hbm, offsets_hbm, forces_hbm, slot_ref, table_ref, out_ref, in_ref,
+    owner_ref, cells_ref, offsets_ref, forces_ref, load_sem, send_sem, recv_sem
+):
+    f32 = jnp.float32
+    loads = [
+        pltpu.make_async_copy(source, target, load_sem.at[k])
+        for k, (source, target) in enumerate(
+            (
+                (owner_hbm, owner_ref), (cells_hbm, cells_ref), (offsets_hbm, offsets_ref),
+                (forces_hbm, forces_ref),
+            )
+        )
+    ]
+    for copy in loads:
+        copy.start()
+    exchange = Exchange(out_ref, in_ref, send_sem, recv_sem)
+    exchange.greet()
+    for copy in loads:
+        copy.wait()
+    markers = owner_ref.shape[1]
+    slots = capacity * exchange.devices
+    owner = owner_ref[...].astype(f32)
+    lanes = lax.broadcasted_iota(jnp.int32, (LANES, markers), 1)
+    rows = lax.broadcasted_iota(jnp.int32, (LANES, markers), 0)
+    before = jnp.zeros((8, markers), f32)
+    for j in range(0, markers, LANES):
+        group = jnp.broadcast_to(owner[:, j : j + LANES], (LANES, LANES))
+        column = jnp.transpose(group)
+        column = jnp.concatenate([column] * (markers // LANES), axis=1)
+        same = jnp.where((column == owner) & (rows + j < lanes), 1.0, 0.0)
+        for k in range(0, LANES, 8):
+            before = before + same[k : k + 8]
+    slot = (owner * capacity + jnp.sum(before, axis=0, keepdims=True)).astype(jnp.int32)
+    slot_ref[...] = slot
+    payload = jnp.concatenate(
+        [
+            cells_ref[...].astype(f32), offsets_ref[...], forces_ref[...],
+            jnp.ones((1, markers), f32), jnp.zeros((6, markers), f32),
+        ],
+        axis=0,
+    )
+    split = thirds(payload)
+    wide = 2 * LANES
+
+    def pack(i, carry):
+        place = lax.broadcasted_iota(jnp.int32, (wide, markers), 0) + i * wide
+        sent = rejoined(transposed_dot(split, flags(place == slot)), 16)
+        for k in range(2):
+            part = sent[:, k * LANES : (k + 1) * LANES]
+            put_tiles(out_ref, 2 * i + k, part[0:8], part[8:16], capacity)
+        return carry
+
+    lax.fori_loop(0, slots // wide, pack, 0)
+    exchange.start()
+    exchange.finish()
+
+    def unpack(i, carry):
+        table_ref[0:8, lanes_of(i)] = block_of(in_ref, i, capacity, 0)
+        table_ref[8:16, lanes_of(i)] = block_of(in_ref, i, capacity, 1)
+        return carry
+
+    lax.fori_loop(0, slots // LANES, unpack, 0)
+
+
+def routed(owner, cells, offsets, forces, capacity):
     devices = lax.axis_size("gx") * lax.axis_size("gy")
-    rows = values.shape[0]
-    tile = 8 * LANES
-    sized = -(-rows * count // tile) * tile
-    flat = values.reshape(rows, devices, count).transpose(1, 0, 2).reshape(devices, rows * count)
-    flat = jnp.pad(flat, ((0, 0), (0, sized - rows * count)))
-    flat = flat.reshape(devices, sized // LANES, LANES)
-    received = pl.pallas_call(
-        exchange_kernel,
-        out_shape=jax.ShapeDtypeStruct(flat.shape, jnp.float32),
-        in_specs=[pl.BlockSpec(memory_space=pltpu.VMEM)],
-        out_specs=pl.BlockSpec(memory_space=pltpu.VMEM),
-        scratch_shapes=[pltpu.SemaphoreType.DMA((devices,)), pltpu.SemaphoreType.DMA((devices,))],
-        compiler_params=pltpu.CompilerParams(collective_id=collective_id, has_side_effects=True),
-    )(flat)
-    received = received.reshape(devices, sized)[:, : rows * count].reshape(devices, rows, count)
-    return received.transpose(1, 0, 2).reshape(rows, devices * count)
+    markers = owner.shape[1]
+    f32 = jnp.float32
+    vmem = pl.BlockSpec(memory_space=pltpu.VMEM)
+    return pl.pallas_call(
+        functools.partial(route_kernel, capacity),
+        out_shape=(
+            jax.ShapeDtypeStruct((1, markers), jnp.int32),
+            jax.ShapeDtypeStruct((16, devices * capacity), f32),
+        ),
+        in_specs=[pl.BlockSpec(memory_space=pltpu.HBM)] * 4,
+        out_specs=[vmem] * 2,
+        scratch_shapes=[pltpu.VMEM((devices, 8, LANES), f32)] * 2
+        + [pltpu.VMEM((1, markers), jnp.int32), pltpu.VMEM((3, markers), jnp.int32)]
+        + [pltpu.VMEM((3, markers), f32)] * 2
+        + [pltpu.SemaphoreType.DMA((4,))]
+        + [pltpu.SemaphoreType.DMA((devices,))] * 2,
+        compiler_params=pltpu.CompilerParams(
+            collective_id=1, has_side_effects=True, vmem_limit_bytes=24 * 1024 * 1024
+        ),
+    )(owner, cells, offsets, forces)
+
+
+def sort_kernel(depth, size_x, received_ref, place_ref, table_ref):
+    f32 = jnp.float32
+    slots = received_ref.shape[1]
+    tiles = depth // LANES
+    blocks = slots // LANES
+    valid = received_ref[9:10] > 0.5
+    start = received_ref[2:3].astype(jnp.int32) - 1
+    bins = jnp.where(start < 0, start + depth, start)
+    bins = jnp.where(valid, lax.shift_right_logical(bins, LANES.bit_length() - 1), tiles)
+    cell = received_ref[0:1].astype(jnp.int32)
+    edge = valid & ((cell < SPREAD_ABOVE) | (cell >= size_x - SPREAD_BELOW))
+    kinds = lax.broadcasted_iota(jnp.int32, (2 * tiles, slots), 0)
+    member = jnp.where(kinds == 2 * bins + jnp.where(edge, 0, 1), 1.0, 0.0)
+    stacked = jnp.concatenate(
+        [member[:, b * LANES : (b + 1) * LANES] for b in range(blocks)], axis=0
+    ).astype(jnp.bfloat16)
+    above = lax.broadcasted_iota(jnp.int32, (LANES, LANES), 0) < lax.broadcasted_iota(
+        jnp.int32, (LANES, LANES), 1
+    )
+    within = jnp.dot(stacked, flags(above), preferred_element_type=f32)
+    sums = jnp.dot(stacked, jnp.ones((LANES, LANES), jnp.bfloat16), preferred_element_type=f32)
+    ranks, run = [], jnp.zeros((2 * tiles, LANES), f32)
+    for b in range(blocks):
+        ranks.append(within[2 * b * tiles : 2 * (b + 1) * tiles] + run)
+        run = run + sums[2 * b * tiles : 2 * (b + 1) * tiles]
+    run = run.astype(jnp.int32)
+    firsts, total = [], jnp.zeros((1, LANES), jnp.int32)
+    lane = lax.broadcasted_iota(jnp.int32, (1, LANES), 1)
+    tile_of, order, edge_total = jnp.zeros_like(total), jnp.zeros_like(total), total
+
+    def chunks_for(amount):
+        return lax.shift_right_logical(amount + (LANES - 1), LANES.bit_length() - 1)
+
+    for k in range(tiles):
+        edges, others = run[2 * k : 2 * k + 1], run[2 * k + 1 : 2 * k + 2]
+        firsts += [total * LANES, total * LANES + edges]
+        edge_chunks = chunks_for(edges)
+        inside = (lane >= edge_total) & (lane < edge_total + edge_chunks)
+        order = jnp.where(inside, total + lane - edge_total, order)
+        edge_total = edge_total + edge_chunks
+        total = total + chunks_for(edges + others)
+        tile_of = tile_of + jnp.where(lane >= total, 1, 0)
+    tile_of = jnp.minimum(tile_of, tiles - 1)
+    order = jnp.where(lane >= edge_total, table_ref.shape[1] // LANES - 1, order)
+    first = jnp.concatenate(firsts, axis=0).astype(f32)
+    spots = jnp.concatenate(
+        [
+            jnp.sum(
+                member[:, b * LANES : (b + 1) * LANES] * (ranks[b] + first), axis=0, keepdims=True
+            )
+            for b in range(blocks)
+        ],
+        axis=1,
+    )
+    place = jnp.where(valid, spots.astype(jnp.int32), -1)
+    place_ref[...] = place
+    count = jnp.max(total.astype(f32)).astype(jnp.int32)
+    payload = jnp.concatenate(
+        [
+            received_ref[0:9], jnp.zeros((7, slots), f32),
+        ],
+        axis=0,
+    )
+    split = thirds(payload)
+    table_ref[...] = jnp.zeros(table_ref.shape, f32)
+    wide = 2 * LANES
+
+    def gather(i, carry):
+        spot = lax.broadcasted_iota(jnp.int32, (wide, slots), 0) + i * wide
+        sorted_part = rejoined(transposed_dot(split, flags(spot == place)), 16)
+        table_ref[:, pl.ds(pl.multiple_of(i * wide, wide), wide)] = sorted_part
+        return carry
+
+    lax.fori_loop(0, lax.div(count + 1, 2), gather, 0)
+    for row, value in enumerate((tile_of, order, edge_total, total)):
+        table_ref[12 + row : 13 + row, 0:LANES] = value.astype(f32)
+
+
+def sorted_table(received, places, depth, size_x):
+    vmem = pl.BlockSpec(memory_space=pltpu.VMEM)
+    return pl.pallas_call(
+        functools.partial(sort_kernel, depth, size_x),
+        out_shape=(
+            jax.ShapeDtypeStruct((1, received.shape[1]), jnp.int32),
+            jax.ShapeDtypeStruct((16, places), jnp.float32),
+        ),
+        in_specs=[vmem],
+        out_specs=[vmem] * 2,
+        compiler_params=pltpu.CompilerParams(vmem_limit_bytes=16 * 1024 * 1024),
+        cost_estimate=pl.CostEstimate(
+            flops=3_000_000_000, bytes_accessed=1_000_000, transcendentals=0
+        ),
+    )(received)
+
+
+def return_kernel(
+    capacity, slot_ref, place_ref, own_ref, low_ref, high_ref, out_values_ref, out_ref, in_ref,
+    marks_ref, back_ref, send_sem, recv_sem
+):
+    f32 = jnp.float32
+    exchange = Exchange(out_ref, in_ref, send_sem, recv_sem)
+    exchange.greet()
+    slots, markers = marks_ref.shape
+    places = own_ref.shape[1]
+    wide = 2 * LANES
+    place = place_ref[...]
+    blank = jnp.zeros((5, wide), f32)
+
+    def unsort(i, total):
+        part = pl.ds(pl.multiple_of(i * wide, wide), wide)
+        values = own_ref[:, part] + low_ref[:, part] + high_ref[:, part]
+        split = thirds(jnp.concatenate([values, blank], axis=0))
+        spot = lax.broadcasted_iota(jnp.int32, (wide, slots), 0) + i * wide
+        return total + jnp.dot(split, flags(spot == place), preferred_element_type=f32)
+
+    total = lax.fori_loop(0, places // wide, unsort, jnp.zeros((24, slots), f32))
+    back_ref[...] = rejoined(total, 8)
+
+    def pack(i, carry):
+        put_tiles(out_ref, i, back_ref[:, lanes_of(i)], None, capacity)
+        return carry
+
+    lax.fori_loop(0, slots // LANES, pack, 0)
+    exchange.start()
+    slot = slot_ref[...]
+
+    def mark(i, carry):
+        rows = pl.ds(pl.multiple_of(i * LANES, LANES), LANES)
+        here = lax.broadcasted_iota(jnp.int32, (LANES, markers), 0) + i * LANES
+        marks_ref[rows, :] = flags(here == slot)
+        return carry
+
+    lax.fori_loop(0, slots // LANES, mark, 0)
+    exchange.finish()
+
+    def unpack(i, carry):
+        back_ref[:, lanes_of(i)] = block_of(in_ref, i, capacity, 0)
+        return carry
+
+    lax.fori_loop(0, slots // LANES, unpack, 0)
+    parts = jnp.dot(thirds(back_ref[...]), marks_ref[...], preferred_element_type=f32)
+    out_values_ref[...] = rejoined(parts, 8)[0:3]
+
+
+def given_back(slot, place, values, low_values, high_values, capacity):
+    devices = lax.axis_size("gx") * lax.axis_size("gy")
+    markers, slots = slot.shape[1], place.shape[1]
+    f32 = jnp.float32
+    vmem = pl.BlockSpec(memory_space=pltpu.VMEM)
+    return pl.pallas_call(
+        functools.partial(return_kernel, capacity),
+        out_shape=jax.ShapeDtypeStruct((3, markers), f32),
+        in_specs=[vmem] * 5,
+        out_specs=vmem,
+        scratch_shapes=[pltpu.VMEM((devices, 8, LANES), f32)] * 2
+        + [pltpu.VMEM((slots, markers), jnp.bfloat16), pltpu.VMEM((8, slots), f32)]
+        + [pltpu.SemaphoreType.DMA((devices,))] * 2,
+        compiler_params=pltpu.CompilerParams(
+            collective_id=2, has_side_effects=True, vmem_limit_bytes=24 * 1024 * 1024
+        ),
+    )(slot, place, values, low_values, high_values)
 
 
 def tent(first, weights, length, wrap=0):
@@ -109,25 +399,43 @@
     return high, low
 
 
-def chunk_tables(part, tile, x_shift, layers, ext_y, depth):
+def chunk_tables(part, tile, x_shift, layers, ext_y, depth, marker_rows):
     cells = part[0:3].astype(jnp.int32)
     table_x = tent(cells[0:1] + x_shift, kernel_weights(part[3:4]), layers)
     table_y = tent(cells[1:2] - 1, kernel_weights(part[4:5]), ext_y, ext_y)
     start = cells[2:3] - 1
     start = jnp.where(start < 0, start + depth, start) - tile * LANES
-    table_z = tent(start, kernel_weights(part[5:6]), 2 * LANES)
+    weights = kernel_weights(part[5:6])
+    if not marker_rows:
+        return table_x, table_y, tent(start, weights, 2 * LANES)
+    packed = jnp.concatenate(
+        [start.astype(jnp.float32), *weights, jnp.zeros((3, LANES), jnp.float32)], axis=0
+    )
+    columns = jnp.transpose(packed)
+    where = lax.broadcasted_iota(jnp.int32, (LANES, 2 * LANES), 1).astype(jnp.float32)
+    where = where - columns[:, 0:1]
+    table_z = jnp.zeros((LANES, 2 * LANES), jnp.float32)
+    for k in range(4):
+        table_z = jnp.where(where == float(k), columns[:, k + 1 : k + 2], table_z)
     return table_x, table_y, table_z
 
 
-def chunk_count(ref):
-    return jnp.max(ref[11:12, 0:LANES]).astype(jnp.int32)
-
-
-def note_tiles(tables, tile_ref):
-    for k, ref in enumerate(tables):
-        for j in range(ref.shape[1] // LANES):
-            tile = jnp.max(ref[10:11, j * LANES : (j + 1) * LANES])
-            tile_ref[k, j] = tile.astype(jnp.int32)
+def chunk_notes(tables, note_ref, note_sem):
+    copies = [
+        pltpu.make_async_copy(ref.at[8:16, 0:LANES], note_ref.at[k], note_sem.at[k])
+        for k, ref in enumerate(tables)
+    ]
+    for copy in copies:
+        copy.start()
+    return copies
+
+
+def note(note_ref, which, row, at):
+    return note_ref[which, row, at].astype(jnp.int32)
+
+
+def note_scratch(tables):
+    return [pltpu.SMEM((tables, 8, LANES), jnp.float32), pltpu.SemaphoreType.DMA((tables,))]
 
 
 def lanes_of(tile):
@@ -145,7 +453,10 @@
 
 
 def spread_kernel(shifts, together, *refs):
-    tables, outs, tile_ref = refs[: len(shifts)], refs[len(shifts) : -1], refs[-1]
+    tables, outs = refs[: len(shifts)], refs[len(shifts) : -2]
+    note_ref, note_sem = refs[-2:]
+    beside = len(tables) > 1
+    copies = chunk_notes(tables, note_ref, note_sem)
 
     def clear(out_ref):
         def body(i, carry):
@@ -157,50 +468,55 @@
 
     for out_ref in outs:
         clear(out_ref)
-    note_tiles(tables, tile_ref)
+    for copy in copies:
+        copy.wait()
 
     def product(which, j):
         ref, out_ref = tables[which], outs[which]
         layers, ext_y, depth = out_ref.shape[1:]
         part = ref[:, lanes_of(j)]
         table_x, table_y, table_z = chunk_tables(
-            part, tile_ref[which, j], shifts[which], padded(layers), ext_y, depth
+            part, note(note_ref, which, 4, j), shifts[which], padded(layers), ext_y, depth, True
         )
         z_high, z_low = halves(table_z)
-        z_pair = jnp.concatenate([z_high, z_high], axis=1)
+        z_pair = jnp.concatenate([z_high, z_high], axis=0)
         planes = []
         for c in range(3):
             pushed = table_x * part[6 + c : 7 + c]
             planes += [pushed[x : x + 1] * table_y for x in range(layers)]
         high, low = halves(jnp.concatenate(planes, axis=0))
-        total = transposed_dot(jnp.concatenate([high, low], axis=1), z_pair)
-        return total + transposed_dot(high, z_low)
+        total = jnp.dot(
+            jnp.concatenate([high, low], axis=1), z_pair, preferred_element_type=jnp.float32
+        )
+        return total + jnp.dot(high, z_low, preferred_element_type=jnp.float32)
 
     def add(which, j, total):
         out_ref = outs[which]
         layers, ext_y, depth = out_ref.shape[1:]
         shape = (3, layers, ext_y, LANES)
-        tile = tile_ref[which, j]
+        tile = note(note_ref, which, 4, j)
         after = lax.rem(tile + 1, depth // LANES)
         out_ref[:, :, :, lanes_of(tile)] += total[:, :LANES].reshape(shape)
         out_ref[:, :, :, lanes_of(after)] += total[:, LANES:].reshape(shape)
 
     def chunk(j, carry):
         kinds = range(len(tables))
-        steps = [(which, together * j + k) for which in kinds for k in range(together)]
+        steps = [
+            (which, note(note_ref, which, 5, j) if beside else together * j + k)
+            for which in kinds
+            for k in range(together)
+        ]
         totals = [product(*step) for step in steps]
         for step, total in zip(steps, totals):
             add(*step, total)
         return carry
 
-    count = chunk_count(tables[0])
-    for ref in tables[1:]:
-        count = jnp.maximum(count, chunk_count(ref))
+    counts = [note(note_ref, which, 6 if beside else 7, 0) for which in range(len(tables))]
+    count = functools.reduce(jnp.maximum, counts)
     lax.fori_loop(0, lax.div(count + (together - 1), together), chunk, 0)
 
 
 def spread_out(tables, shifts, layers, together, ext_y, depth, cost):
-    chunks = tables[0].shape[1] // LANES
     return pl.pallas_call(
         functools.partial(spread_kernel, shifts, together),
         out_shape=[
@@ -208,7 +524,7 @@
         ],
         in_specs=[pl.BlockSpec(memory_space=pltpu.VMEM)] * len(tables),
         out_specs=[pl.BlockSpec(memory_space=pltpu.VMEM)] * len(tables),
-        scratch_shapes=[pltpu.SMEM((len(tables), chunks), jnp.int32)],
+        scratch_shapes=note_scratch(len(tables)),
         compiler_params=pltpu.CompilerParams(vmem_limit_bytes=24 * 1024 * 1024),
         cost_estimate=pl.CostEstimate(flops=cost, bytes_accessed=1_000_000, transcendentals=0),
     )(*tables)
@@ -440,7 +756,7 @@
     layers = size_x + 2
     tiles = depth // LANES
     f32 = jnp.float32
-    vmem, hbm = pl.BlockSpec(memory_space=pltpu.VMEM), pl.BlockSpec(memory_space=pl.ANY)
+    vmem, hbm = pl.BlockSpec(memory_space=pltpu.VMEM), pl.BlockSpec(memory_space=pltpu.HBM)
     return pl.pallas_call(
         smoothing_kernel,
         out_shape=jax.ShapeDtypeStruct((3, size_x, ext_y, depth), f32),
@@ -465,7 +781,7 @@
             pltpu.SemaphoreType.DMA((24,)),
         ],
         compiler_params=pltpu.CompilerParams(
-            collective_id=0, has_side_effects=True, vmem_limit_bytes=36 * 1024 * 1024
+            collective_id=0, has_side_effects=True, vmem_limit_bytes=32 * 1024 * 1024
         ),
     )(own, below, above, velocity, viscosity, vel_low, vel_high)
 
@@ -474,7 +790,7 @@
     layers, ext_y, depth = high_of.shape[1:]
     after = lax.rem(tile + 1, depth // LANES)
     table_x, table_y, table_z = chunk_tables(
-        ref[:, lanes_of(j)], tile, x_shift, padded(layers), ext_y, depth
+        ref[:, lanes_of(j)], tile, x_shift, padded(layers), ext_y, depth, False
     )
     z_high, z_low = halves(table_z)
     z_pair = jnp.concatenate([z_high, z_low], axis=1)
@@ -504,8 +820,9 @@
         target[c : c + 1, lanes_of(j)] = jnp.sum(total, axis=0, keepdims=True)
 
 
-def sample_kernel(table_ref, field_ref, vel_ref, out_ref, field_high, field_low, tile_ref):
+def sample_kernel(table_ref, field_ref, vel_ref, out_ref, field_high, field_low, note_ref, note_sem):
     size_x, size_y = vel_ref.shape[1:3]
+    copies = chunk_notes([table_ref], note_ref, note_sem)
 
     def split(x, carry):
         for c in range(3):
@@ -515,14 +832,16 @@
         return carry
 
     lax.fori_loop(0, size_x, split, 0)
-    note_tiles([table_ref], tile_ref)
+    copies[0].wait()
+    out_ref[...] = jnp.zeros(out_ref.shape, jnp.float32)
 
     def chunk(i, carry):
         for j in (2 * i, 2 * i + 1):
-            sample_chunk(table_ref, tile_ref[0, j], j, out_ref, -1, field_high, field_low)
-        return carry
-
-    lax.fori_loop(0, lax.div(chunk_count(table_ref) + 1, 2), chunk, 0)
+            tile = note(note_ref, 0, 4, j)
+            sample_chunk(table_ref, tile, j, out_ref, -1, field_high, field_low)
+        return carry
+
+    lax.fori_loop(0, lax.div(note(note_ref, 0, 7, 0) + 1, 2), chunk, 0)
 
 
 def sampled(table, field, size_y):
@@ -538,7 +857,7 @@
         in_specs=[vmem] * 2,
         out_specs=[vmem] * 2,
         scratch_shapes=[pltpu.VMEM((3, size_x, ext_y, depth), jnp.bfloat16)] * 2
-        + [pltpu.SMEM((1, table.shape[1] // LANES), jnp.int32)],
+        + note_scratch(1),
         compiler_params=pltpu.CompilerParams(vmem_limit_bytes=28 * 1024 * 1024),
         cost_estimate=pl.CostEstimate(
             flops=10_000_000_000, bytes_accessed=1_000_000, transcendentals=0
@@ -548,23 +867,30 @@
 
 def sample_beside_kernel(
     low_ref, high_ref, field_ref, low_out, high_out, first_high, first_low, last_high, last_low,
-    tile_ref
+    note_ref, note_sem
 ):
     size_x = field_ref.shape[1]
+    copies = chunk_notes([low_ref, high_ref], note_ref, note_sem)
     for c in range(3):
         for x in range(2):
             first_high[c, x], first_low[c, x] = halves(field_ref[c, x])
         last_high[c, 0], last_low[c, 0] = halves(field_ref[c, size_x - 1])
-    note_tiles([low_ref, high_ref], tile_ref)
-
-    def chunk(j, carry):
-        sample_chunk(
-            low_ref, tile_ref[0, j], j, low_out, -size_x - 1, first_high, first_low
-        )
-        sample_chunk(high_ref, tile_ref[1, j], j, high_out, 0, last_high, last_low)
-        return carry
-
-    lax.fori_loop(0, jnp.maximum(chunk_count(low_ref), chunk_count(high_ref)), chunk, 0)
+    for copy in copies:
+        copy.wait()
+    low_out[...] = jnp.zeros(low_out.shape, jnp.float32)
+    high_out[...] = jnp.zeros(high_out.shape, jnp.float32)
+
+    def chunk(i, carry):
+        j = note(note_ref, 0, 5, i)
+        tile = note(note_ref, 0, 4, j)
+        sample_chunk(low_ref, tile, j, low_out, -size_x - 1, first_high, first_low)
+        j = note(note_ref, 1, 5, i)
+        tile = note(note_ref, 1, 4, j)
+        sample_chunk(high_ref, tile, j, high_out, 0, last_high, last_low)
+        return carry
+
+    count = jnp.maximum(note(note_ref, 0, 6, 0), note(note_ref, 1, 6, 0))
+    lax.fori_loop(0, count, chunk, 0)
 
 
 def sampled_beside(low, high, field):
@@ -577,33 +903,12 @@
         out_specs=[vmem] * 2,
         scratch_shapes=[pltpu.VMEM((3, 2, ext_y, depth), jnp.bfloat16)] * 2
         + [pltpu.VMEM((3, 1, ext_y, depth), jnp.bfloat16)] * 2
-        + [pltpu.SMEM((2, low.shape[1] // LANES), jnp.int32)],
+        + note_scratch(2),
         compiler_params=pltpu.CompilerParams(vmem_limit_bytes=16 * 1024 * 1024),
         cost_estimate=pl.CostEstimate(
             flops=2_000_000_000, bytes_accessed=1_000_000, transcendentals=0
         ),
     )(low, high, field)
-
-
-def ranked(onehot):
-    members, kinds = onehot.shape
-    group = min(128, members)
-    blocks = onehot.reshape(members // group, group, kinds)
-    lower = (
-        lax.broadcasted_iota(jnp.int32, (group, group), 0)
-        > lax.broadcasted_iota(jnp.int32, (group, group), 1)
-    ).astype(jnp.float32)
-    within = jnp.einsum("ij,bjd->bid", lower, blocks)
-    totals = jnp.sum(blocks, axis=1)
-    before = jnp.cumsum(totals, axis=0) - totals
-    rank = jnp.sum((within + before[:, None, :]) * blocks, axis=-1).reshape(members)
-    return rank.astype(jnp.int32), jnp.sum(totals, axis=0).astype(jnp.int32)
-
-
-def onehot_of(index, kinds):
-    return (index[:, None] == lax.broadcasted_iota(jnp.int32, (index.shape[0], kinds), 1)).astype(
-        jnp.float32
-    )
 
 
 def stepped(velocity, viscosity, cells, offsets, forces, owners):
@@ -617,53 +922,27 @@
     ext_y = -(-(size_y + 3) // 8) * 8
     tiles = depth // LANES
 
-    owner = owners[:, 0]
-    rank, _ = ranked(onehot_of(owner, devices))
-    slot = owner * capacity + rank
-    payload = jnp.concatenate(
-        [cells.astype(jnp.float32), offsets, forces, jnp.ones((1, markers), jnp.float32)], axis=0
-    )
-    outgoing = jnp.zeros((10, slots), jnp.float32).at[:, slot].set(payload, unique_indices=True)
-    received = exchanged(outgoing, capacity, 1)
-    edges = (velocity[:, size_x - 1 :], velocity[:, 0:1])
-    received, edges = lax.optimization_barrier((received, edges))
-    vel_low = shifted(edges[0], "gx", 1)
-    vel_high = shifted(edges[1], "gx", -1)
-
-    valid = received[9] > 0.5
-    start = received[2].astype(jnp.int32) - 1
-    bins = jnp.where(start < 0, start + depth, start) // LANES
-    bins = jnp.where(valid, bins, tiles)
+    slot, received = routed(owners.reshape(1, markers), cells, offsets, forces, capacity)
+    received, edge = lax.optimization_barrier((received, velocity[:, size_x - 1 :]))
+    vel_low = shifted(edge, "gx", 1)
     chunks = -(-(slots // LANES + tiles) // 2) * 2
-    places = chunks * LANES
-    rank, totals = ranked(onehot_of(bins, tiles))
-    needed = (totals + (LANES - 1)) // LANES
-    ends = jnp.cumsum(needed)
-    first = ends - needed
-    shift = jnp.sum(jnp.where(bins[:, None] == jnp.arange(tiles)[None, :], first[None, :], 0), axis=1)
-    spot = jnp.where(valid, shift * LANES + rank, places)
-    count = jnp.full((slots,), ends[-1].astype(jnp.float32))
-    sorting = jnp.concatenate([received, jnp.stack([bins.astype(jnp.float32), count])], axis=0)
-    own = jnp.zeros((12, places), jnp.float32).at[:, spot].set(
-        sorting, mode="drop", unique_indices=True
-    )
+    place, own = sorted_table(received, chunks * LANES, depth, size_x)
+    own, edge = lax.optimization_barrier((own, velocity[:, 0:1]))
     low = shifted(own, "gx", 1)
     high = shifted(own, "gx", -1)
-
+    vel_high = shifted(edge, "gx", -1)
     (spread,) = spread_out([own], (0,), (size_x + 2,), 2, ext_y, depth, 10_000_000_000)
     below, above = spread_out(
-        [low, high], (-size_x, 0), (3, 2), 1, ext_y, depth, 2_000_000_000,
+        [low, high], (-size_x, 0), (SPREAD_BELOW, SPREAD_ABOVE), 1, ext_y, depth,
+        2_000_000_000,
     )
     field = smoothed(spread, below, above, velocity, viscosity, vel_low, vel_high)
     low_values, high_values = sampled_beside(low, high, field)
     low_values = shifted(low_values, "gx", -1)
     high_values = shifted(high_values, "gx", 1)
     new_velocity, values = sampled(own, field, size_y)
-    values = values + low_values + high_values
-    back = values[:, jnp.minimum(spot, places - 1)]
-    back = jnp.where(valid[None], back, 0.0)
-    returned = exchanged(back, capacity, 2)
-    return (new_velocity, returned[:, slot])
+    marker_velocity = given_back(slot, place, values, low_values, high_values, capacity)
+    return (new_velocity, marker_velocity)
 
 
 def solution(mesh):

time: 163 us -> 131 us (0.80)
  local copies, waits for them, and re-layouts: 32.4 us -> 4.65 us
  waiting for transfers between devices: 3.73 us -> 7.66 us
  other arithmetic: 3.87 us -> 0.01 us
  Pallas kernels: 111 us -> 108 us
    scatter x3 -> x0, local copies, waits for them, and re-layouts: 9.8 us -> none  [the longest x2 6.46 us: stepped(): jnp.zeros((12, places), jnp.float32).at[:, spot]]
    gather x3 -> x0, local copies, waits for them, and re-layouts: 8.66 us -> none  [the longest x2 5.85 us: stepped(): back = values[:, jnp.minimum(spot, places - 1)]]
    pallas_call x2 -> x3, Pallas kernels: 28.2 us -> 34.2 us  [the longest x1 17.9 us: given_back(): pl.pallas_call(functools.partial(return_kernel, capacity), out_shape=jax....]
    unnamed x15, local copies, waits for them, and re-layouts: 8.75 us -> 3.46 us
    pallas_call x1, Pallas kernels: 53.9 us -> 49.7 us  [smoothed(): pl.pallas_call(smoothing_kernel, out_shape=jax.ShapeDtypeStruct((3, size_...]
    ppermute x6, waiting for transfers between devices: 3.73 us -> 7.66 us  [shifted(): lax.ppermute(block, axis, [(i, (i + step) % count) for i in range(count)])]
    pallas_call x1, Pallas kernels: 6.44 us -> 3.49 us  [sampled_beside(): pl.pallas_call(sample_beside_kernel, out_shape=[jax.ShapeDtypeStruct((3,...]
  transfers between devices with their start and end apart: 6 -> 6, of which waited for: 1 -> 2; matrix products, arithmetic and copies ran while one was open for 0% -> 0% of each run, Pallas kernels for 14% -> 16%
where the time goes in v1:
time: 131 us; the launch traced here: 130 us
  Pallas kernels  108 us (82%)
  starting transfers between devices  8.52 us (7%)
  waiting for transfers between devices  7.66 us (6%)
  local copies, waits for them, and re-layouts  4.65 us (4%)
    pallas_call x1, Pallas kernels, smoothed(): pl.pallas_call(smoothing_kernel, out_shape=jax.ShapeDtypeStruct((3, size_...  49.7 us
    pallas_call x1, Pallas kernels, given_back(): pl.pallas_call(functools.partial(return_kernel, capacity), out_shape=jax....  17.9 us
    pallas_call x2, Pallas kernels, spread_out(): pl.pallas_call(functools.partial(spread_kernel, shifts, together), out_sh...  14.4 us
    pallas_call x1, Pallas kernels, routed(): pl.pallas_call(functools.partial(route_kernel, capacity), out_shape=(jax....  14.3 us
    ppermute x6, starting transfers between devices, shifted(): lax.ppermute(block, axis, [(i, (i + step) % count) for i in range(count)])  8.52 us
    ppermute x6, waiting for transfers between devices, shifted(): lax.ppermute(block, axis, [(i, (i + step) % count) for i in range(count)])  7.66 us
    pallas_call x1, Pallas kernels, sampled(): pl.pallas_call(sample_kernel, out_shape=(jax.ShapeDtypeStruct((3, size_x,...  6.57 us
    pallas_call x1, Pallas kernels, sampled_beside(): pl.pallas_call(sample_beside_kernel, out_shape=[jax.ShapeDtypeStruct((3,...  3.49 us
  transfers between devices with their start and end apart: 6, of which 2 were waited for; matrix products, arithmetic and copies ran while one was open for 0% of the time, Pallas kernels for 16%

profile of v1, /device:TPU:0, one launch (start us, length us, event | category | flops | bytes accessed | tf_op | source)
XLA Modules:
  0.0 130.0 jit_solution(10671334916527282949)
XLA Ops:
  0.6 1.2 fusion
  1.8 0.0 copy-start.1
  1.8 0.7 copy-done.1
  2.5 0.0 copy-start.2
  2.5 0.7 copy-done.2
  3.3 0.0 copy-start.3
  3.3 0.7 copy-done.3
  4.0 0.0 copy-start.4
  4.0 0.7 copy-done.4
  4.7 14.3 %shard_map.77 = (s32[1,1024]{1,0:T(1,128)S(1)}, f32[16,2048]{1,0:T(8,128)S(1)}) custom-call(s32[1,1024]{1,0:T(1,128)S(1)} %bitcast.3, s32[3,1024]{1,0:T(4,128)S(1)} %copy-done.1, f32[3,1024]{1,0:T(4,128)S(1)} %copy-done.2, f32[3,1024]{1,0:T(4,128)S(1)} %copy-done.3), custom_call_target="tpu_custom_call" | custom-call | tf_op jit(solution)/shard_map/pallas_call | solution.py:202
  18.9 0.0 slice-start
  19.0 2.1 %shard_map.78 = (s32[1,2048]{1,0:T(1,128)S(1)}, f32[16,3072]{1,0:T(8,128)S(1)}) custom-call(f32[16,2048]{1,0:T(8,128)S(1)} %get-tuple-element.17.received_ref), custom_call_target="tpu_custom_call" | custom-call | flops 3000000000 | bytes 1000000 | tf_op jit(solution)/shard_map/pallas_call | solution.py:301
  21.0 0.0 slice-start.1
  21.0 3.5 %collective-permute-start.1 = (f32[16,3072]{1,0:T(8,128)S(1)}, f32[16,3072]{1,0:T(8,128)S(1)}, u32[]{:S(2)}, u32[]{:S(2)}) collective-permute-start(f32[16,3072]{1,0:T(8,128)S(1)} %get-tuple-element.19.refs_0_.table_ref), channel_id=1, source_target_pairs={{0,24},{8,0},{16,8},{24,16},{1,25},{9,1},{17,9},{25,17},{2,26},{10... | collective-permute-start | bytes 589832 | tf_op jit(solution)/shard_map/ppermute | solution.py:21
  24.5 0.0 collective-permute-start
  24.5 2.9 %collective-permute-start.3 = (f32[3,1,28,1024]{3,2,1,0:T(8,128)S(1)}, f32[3,1,28,1024]{3,2,1,0:T(8,128)S(1)}, u32[]{:S(2)}, u32[]{:S(2)}) collective-permute-start(f32[3,1,28,1024]{3,2,1,0:T(8,128)S(1)} %get-tuple-element.23), channel_id=1, source_target_pairs={{0,24},{8,0},{16,8},{24,16},{1,25},{9,1},{17,9},{25,17},{2,26},{10... | collective-permute-start | bytes 1032200 | tf_op jit(solution)/shard_map/ppermute | solution.py:21
  27.5 0.0 collective-permute-start.2
  27.5 7.8 %shard_map.79.own_ref = f32[3,14,32,1024]{3,2,1,0:T(8,128)S(1)} custom-call(f32[16,3072]{1,0:T(8,128)S(1)} %get-tuple-element.19.refs_0_.table_ref), custom_call_target="tpu_custom_call" | custom-call | flops 10000000000 | bytes 1000000 | tf_op jit(solution)/shard_map/pallas_call | solution.py:520
  35.2 0.0 copy-start
  35.3 0.0 collective-permute-done.1.refs_1_.high_ref
  35.3 0.0 collective-permute-done.refs_0_.low_ref
  35.3 6.7 %shard_map.80 = (f32[3,3,32,1024]{3,2,1,0:T(8,128)S(1)}, f32[3,2,32,1024]{3,2,1,0:T(8,128)S(1)}) custom-call(f32[16,3072]{1,0:T(8,128)S(1)} %collective-permute-done.refs_0_.low_ref, f32[16,3072]{1,0:T(8,128)S(1)} %collective-permute-done.1.refs_1_.high_ref), custom_call_target="tpu_custom_call" | custom-call | flops 2000000000 | bytes 1000000 | tf_op jit(solution)/shard_map/pallas_call | solution.py:520
  42.0 0.5 collective-permute-done.3.vel_high
  42.5 7.1 %collective-permute-done.2.vel_low = f32[3,1,28,1024]{3,2,1,0:T(8,128)S(1)} collective-permute-done((f32[3,1,28,1024]{3,2,1,0:T(8,128)S(1)}, f32[3,1,28,1024]{3,2,1,0:T(8,128)S(1)}, u32[]{:S(2)}, u32[]{:S(2)}) %collective-permute-start.2) | collective-permute-done | bytes 344096 | tf_op jit(solution)/shard_map/ppermute | solution.py:21
  49.6 0.0 slice-done
  49.6 0.0 slice-done.1
  49.6 0.0 copy-done
  49.6 49.7 %shard_map.81.field_ref = f32[3,12,32,1024]{3,2,1,0:T(8,128)S(1)} custom-call(f32[3,14,32,1024]{3,2,1,0:T(8,128)S(1)} %shard_map.79.own_ref, f32[3,3,32,1024]{3,2,1,0:T(8,128)S(1)} %get-tuple-element.20.below_ref, f32[3,2,32,1024]{3,2,1,0:T(8,128)S(1)} %get-tuple-element.21.above_ref, f32[3,12,28,1024]{3,2,1,0:T(8,128)S(1)} %bitcast.2, ...), custom_call_target="tpu_custom_call" | custom-call | tf_op jit(solution)/shard_map/pallas_call | solution.py:760
  99.3 3.5 %shard_map.83 = (f32[3,3072]{1,0:T(4,128)S(1)}, f32[3,3072]{1,0:T(4,128)S(1)}) custom-call(f32[16,3072]{1,0:T(8,128)S(1)} %collective-permute-done.refs_0_.low_ref, f32[16,3072]{1,0:T(8,128)S(1)} %collective-permute-done.1.refs_1_.high_ref, f32[3,12,32,1024]{3,2,1,0:T(8,128)S(1)} %shard_map.81.field_ref), custom_call_target="tpu_custom_call" | custom-call | flops 2000000000 | bytes 1000000 | tf_op jit(solution)/shard_map/pallas_call | solution.py:899
  102.8 1.9 %collective-permute-start.4 = (f32[3,3072]{1,0:T(4,128)S(1)}, f32[3,3072]{1,0:T(4,128)S(1)}, u32[]{:S(2)}, u32[]{:S(2)}) collective-permute-start(f32[3,3072]{1,0:T(4,128)S(1)} %get-tuple-element.28), channel_id=1, source_target_pairs={{0,24},{8,0},{16,8},{24,16},{1,25},{9,1},{17,9},{25,17},{2,26},{10... | collective-permute-start | bytes 110600 | tf_op jit(solution)/shard_map/ppermute | solution.py:21
  104.7 0.2 collective-permute-start.5
  104.9 6.6 %shard_map.82 = (f32[3,12,28,1024]{3,2,1,0:T(8,128)}, f32[3,3072]{1,0:T(4,128)S(1)}) custom-call(f32[16,3072]{1,0:T(8,128)S(1)} %get-tuple-element.19.refs_0_.table_ref, f32[3,12,32,1024]{3,2,1,0:T(8,128)S(1)} %shard_map.81.field_ref), custom_call_target="tpu_custom_call" | custom-call | flops 10000000000 | bytes 1000000 | tf_op jit(solution)/shard_map/pallas_call | solution.py:851
  111.5 0.0 collective-permute-done.4.low_ref
  111.5 0.0 collective-permute-done.5.high_ref
  111.5 17.9 %shard_map.84 = f32[3,1024]{1,0:T(4,128)S(1)} custom-call(s32[1,1024]{1,0:T(1,128)S(1)} %get-tuple-element.25.slot_ref, s32[1,2048]{1,0:T(1,128)S(1)} %get-tuple-element.26.place_ref, f32[3,3072]{1,0:T(4,128)S(1)} %get-tuple-element.27.own_ref, f32[3,3072]{1,0:T(4,128)S(1)} %collective-permute-done.4.low_ref, f32[3,3072]{1,0:T(4,128)S(1)} %collective-permute-done.5.high_ref), custom_call_target="tpu_custom_call" | custom-call | tf_op jit(solution)/shard_map/pallas_call | solution.py:370
  129.4 0.6 copy.9
  (1 shorter events, 0.0 us)
Async XLA Ops:
  1.8 0.7 copy-start.1
  2.5 0.7 copy-start.2
  3.3 0.7 copy-start.3
  4.0 0.7 copy-start.4
  18.9 30.6 %slice-start = ((s8[4718592]{0:T(1024)(128)(4,1)}), s8[4194304]{0:T(1024)(128)(4,1)S(1)}, s32[]{:S(2)}) async-start(s8[4718592]{0:T(1024)(128)(4,1)} %bitcast.1), calls=%async_computation | async-start | bytes 8388608
  21.0 28.6 %slice-start.1 = ((s8[4718592]{0:T(1024)(128)(4,1)}), s8[524288]{0:T(1024)(128)(4,1)S(1)}, s32[]{:S(2)}) async-start(s8[4718592]{0:T(1024)(128)(4,1)} %bitcast.1), calls=%async_computation.1 | async-start | bytes 1048576
  21.0 14.2 %collective-permute-start.1 = (f32[16,3072]{1,0:T(8,128)S(1)}, f32[16,3072]{1,0:T(8,128)S(1)}, u32[]{:S(2)}, u32[]{:S(2)}) collective-permute-start(f32[16,3072]{1,0:T(8,128)S(1)} %get-tuple-element.19.refs_0_.table_ref), channel_id=1, source_target_pairs={{0,24},{8,0},{16,8},{24,16},{1,25},{9,1},{17,9},{25,17},{2,26},{10... | collective-permute-start | bytes 589832 | tf_op jit(solution)/shard_map/ppermute | solution.py:21
  24.5 10.8 %collective-permute-start = (f32[16,3072]{1,0:T(8,128)S(1)}, f32[16,3072]{1,0:T(8,128)S(1)}, u32[]{:S(2)}, u32[]{:S(2)}) collective-permute-start(f32[16,3072]{1,0:T(8,128)S(1)} %get-tuple-element.19.refs_0_.table_ref), channel_id=1, source_target_pairs={{0,8},{8,16},{16,24},{24,0},{1,9},{9,17},{17,25},{25,1},{2,10},{10... | collective-permute-start | bytes 589832 | tf_op jit(solution)/shard_map/ppermute | solution.py:21
  24.5 17.9 %collective-permute-start.3 = (f32[3,1,28,1024]{3,2,1,0:T(8,128)S(1)}, f32[3,1,28,1024]{3,2,1,0:T(8,128)S(1)}, u32[]{:S(2)}, u32[]{:S(2)}) collective-permute-start(f32[3,1,28,1024]{3,2,1,0:T(8,128)S(1)} %get-tuple-element.23), channel_id=1, source_target_pairs={{0,24},{8,0},{16,8},{24,16},{1,25},{9,1},{17,9},{25,17},{2,26},{10... | collective-permute-start | bytes 1032200 | tf_op jit(solution)/shard_map/ppermute | solution.py:21
  27.5 22.1 %collective-permute-start.2 = (f32[3,1,28,1024]{3,2,1,0:T(8,128)S(1)}, f32[3,1,28,1024]{3,2,1,0:T(8,128)S(1)}, u32[]{:S(2)}, u32[]{:S(2)}) collective-permute-start(f32[3,1,28,1024]{3,2,1,0:T(8,128)S(1)} %get-tuple-element.22), channel_id=1, source_target_pairs={{0,8},{8,16},{16,24},{24,0},{1,9},{9,17},{17,25},{25,1},{2,10},{10... | collective-permute-start | bytes 1032200 | tf_op jit(solution)/shard_map/ppermute | solution.py:21
  35.2 14.4 %copy-start = (f32[12,28,1024]{2,1,0:T(8,128)S(1)}, f32[12,28,1024]{2,1,0:T(8,128)}, u32[]{:S(2)}) copy-start(f32[12,28,1024]{2,1,0:T(8,128)} %visc_hbm.1) | copy-start | bytes 4128772
  102.8 8.7 %collective-permute-start.4 = (f32[3,3072]{1,0:T(4,128)S(1)}, f32[3,3072]{1,0:T(4,128)S(1)}, u32[]{:S(2)}, u32[]{:S(2)}) collective-permute-start(f32[3,3072]{1,0:T(4,128)S(1)} %get-tuple-element.28), channel_id=1, source_target_pairs={{0,24},{8,0},{16,8},{24,16},{1,25},{9,1},{17,9},{25,17},{2,26},{10... | collective-permute-start | bytes 110600 | tf_op jit(solution)/shard_map/ppermute | solution.py:21
  104.7 6.8 %collective-permute-start.5 = (f32[3,3072]{1,0:T(4,128)S(1)}, f32[3,3072]{1,0:T(4,128)S(1)}, u32[]{:S(2)}, u32[]{:S(2)}) collective-permute-start(f32[3,3072]{1,0:T(4,128)S(1)} %get-tuple-element.29), channel_id=1, source_target_pairs={{0,8},{8,16},{16,24},{24,0},{1,9},{9,17},{17,25},{25,1},{2,10},{10... | collective-permute-start | bytes 110600 | tf_op jit(solution)/shard_map/ppermute | solution.py:21
